TPU v7x, 32 devices: a whole 2x2x4 slice. The times are simulated.
32 devices in a mesh: groups: 2 (over y), vocab: 16 (over z, x, core).
Axes of the slice: x: 2, y: 2, z: 4, core: 2. Of those that a mesh axis runs over, the one named last changes fastest.
Arguments:
- hidden: bfloat16 [512, 1280], P(('groups', 'vocab')), parts along dimension 0, may hold values from -320 to 320
- embedding: bfloat16 [6144, 1280], P('vocab'), may hold values from -0.15625 to 0.15625
- prev_tokens: int32 [2, 512], P(None, 'groups'), parts along dimension 1, may hold values from 0 to 6143, as said below
- last_stamp: int32 [512], P('groups'), parts along dimension 0, may hold values from -1 to 1500, as said below
- sample_begin: int32 [512], P('groups'), parts along dimension 0, may hold values from 1 to 4
- seq_length: int32 [512], P('groups'), parts along dimension 0, may hold values from 1 to 9, as said below
- chosen: int32 [5, 512], P(None, 'groups'), parts along dimension 1, may hold values from 0 to 6143
Outputs:
- picked_logprob: float32 [5, 512], P(None, ('groups', 'vocab')), parts along dimension 1
- stamp_logprob: float32 [512], P(('groups', 'vocab')), parts along dimension 0
There are 2 independent parts, one for each index of `groups`. A program takes and returns all parts, laid end to end along the dimension named above; an argument that names none is the same for every part. Nothing has to cross between parts.
Inputs may be any that keep to these rules, and one draw needn't show every extreme that they name: prev_tokens[1, r] is row r's latest token and prev_tokens[0, r] the one before; ids at or above 4643 are timestamps. `last_stamp`: index among the 1501 timestamps of the latest timestamp token sampled since the row's sample begin, -1 if none; equal to the latest token's index when that token is a timestamp and was sampled. `seq_length`: at least the row's sample_begin and at most sample_begin + 5.
All inputs are finite; a program needn't handle non-finite values.
Results may differ from a plain program's by a relative error of at most 0.0003.
Values may be sent and summed in bfloat16 or wider, within the bound.
No kernel may reach another device: no remote copies, remote signals or barrier semaphores. Data moves between devices by JAX's collectives and lax.ppermute only.
A program may use at most 64 MiB of HBM per device.

v0:
```python
import math

import jax
import jax.numpy as jnp
from jax import lax
from jax.sharding import PartitionSpec as P

TSN = 1501
SPECIALS = 108
INITIAL = 50


MASK_VALUE = -1000000000.0
EMPTY_VALUE = -3000000000.0
SLOPE = 4.0
FLOOR = -30.0


def rule_mask(columns, prev_tokens, last_stamp, sample_begin, seq_length, stamp_begin):
    generated = seq_length - sample_begin
    last_is = (generated >= 1) & (prev_tokens[1] >= stamp_begin)
    before_is = (generated < 2) | (prev_tokens[0] >= stamp_begin)
    column = columns[None, :]
    is_stamp = column >= stamp_begin
    offset = column - stamp_begin
    masked = column == stamp_begin - 1
    masked = masked | (last_is & before_is)[:, None] & is_stamp
    masked = masked | (last_is & ~before_is)[:, None] & (column < stamp_begin - SPECIALS)
    bound = last_stamp + jnp.where(last_is & ~before_is, 0, 1).astype(jnp.int32)
    masked = masked | is_stamp & (offset < bound[:, None]) & (last_stamp >= 0)[:, None]
    begin = (generated == 0)[:, None]
    masked = masked | begin & (column < stamp_begin)
    masked = masked | begin & is_stamp & (offset > INITIAL)
    return masked


def finalize(text_max, text_total, stamp_max, stamp_total, picked, chosen, stamp_begin):
    text_lse = text_max + jnp.log(text_total)
    stamp_lse = stamp_max + jnp.log(stamp_total)
    penalty = SLOPE * jnp.maximum(stamp_lse - text_max, 0.0)
    shifted = text_lse - penalty
    larger = jnp.maximum(shifted, stamp_lse)
    total = larger + jnp.log(jnp.exp(shifted - larger) + jnp.exp(stamp_lse - larger))
    adjusted = picked - jnp.where(chosen < stamp_begin, penalty[None, :], 0.0) - total[None, :]
    return (jnp.maximum(adjusted, FLOOR), jnp.maximum(stamp_lse - total, FLOOR))


def block_stats(
    rows, table, columns, is_text, prev, stamp, begin, length, local_pick, owned, stamp_begin
):
    logits = lax.dot_general(
        rows, table, (((1,), (1,)), ((), ())), preferred_element_type=jnp.float32
    )
    masked = rule_mask(columns, prev, stamp, begin, length, stamp_begin)
    values = jnp.where(masked, MASK_VALUE, logits)
    text_max = jnp.max(jnp.where(is_text, values, EMPTY_VALUE), axis=1)
    text_total = jnp.sum(jnp.where(is_text, jnp.exp(values - text_max[:, None]), 0.0), axis=1)
    stamp_max = jnp.max(jnp.where(is_text, EMPTY_VALUE, values), axis=1)
    stamp_total = jnp.sum(jnp.where(is_text, 0.0, jnp.exp(values - stamp_max[:, None])), axis=1)
    found = jnp.take_along_axis(values, local_pick.T, axis=1).T
    picked = jnp.where(owned, found, 0.0)
    return (text_max, text_total, stamp_max, stamp_total, picked)


def per_device(hidden, embedding, prev_tokens, last_stamp, sample_begin, seq_length, chosen):
    width = embedding.shape[0]
    row_dev = hidden.shape[0]
    count = lax.axis_size("vocab")
    index = lax.axis_index("vocab")
    stamp_begin = width * count - TSN
    first_column = index * width
    columns = first_column + lax.iota(jnp.int32, width)
    is_text = columns < stamp_begin
    nsel = chosen.shape[0]
    piece = lax.all_gather(hidden, "vocab", axis=0, tiled=True)
    rows_here = piece.shape[0]
    block = math.gcd(rows_here, 512)

    def one_block(number):
        begin_at = number * block
        inner = number * block
        pick = lax.dynamic_slice_in_dim(chosen, begin_at, block, 1)
        owned = (pick >= first_column) & (pick < first_column + width)
        local = jnp.clip(pick - first_column, 0, width - 1)
        result = block_stats(
            lax.dynamic_slice_in_dim(piece, inner, block, 0),
            embedding,
            columns,
            is_text,
            lax.dynamic_slice_in_dim(prev_tokens, begin_at, block, 1),
            lax.dynamic_slice_in_dim(last_stamp, begin_at, block, 0),
            lax.dynamic_slice_in_dim(sample_begin, begin_at, block, 0),
            lax.dynamic_slice_in_dim(seq_length, begin_at, block, 0),
            local,
            owned,
            stamp_begin,
        )
        return jnp.concatenate([jnp.stack(result[:4]), result[4]], axis=0)

    stacked = lax.map(one_block, jnp.arange(rows_here // block, dtype=jnp.int32))
    stats = jnp.transpose(stacked, (1, 0, 2)).reshape(4 + nsel, rows_here)
    text_max = stats[0]
    text_total = stats[1]
    stamp_max = stats[2]
    stamp_total = stats[3]
    picked = stats[4:]
    own = index * row_dev
    own_chosen = lax.dynamic_slice_in_dim(chosen, own, row_dev, 1)
    text_top, stamp_top = lax.pmax((text_max, stamp_max), "vocab")
    text_sum, stamp_sum = lax.psum(
        (text_total * jnp.exp(text_max - text_top), stamp_total * jnp.exp(stamp_max - stamp_top)),
        "vocab",
    )
    picked_own = lax.psum_scatter(picked, "vocab", scatter_dimension=1, tiled=True)
    text_own = lax.dynamic_slice_in_dim(text_top, own, row_dev, 0)
    text_sum_own = lax.dynamic_slice_in_dim(text_sum, own, row_dev, 0)
    stamp_own = lax.dynamic_slice_in_dim(stamp_top, own, row_dev, 0)
    stamp_sum_own = lax.dynamic_slice_in_dim(stamp_sum, own, row_dev, 0)
    return finalize(
        text_own, text_sum_own, stamp_own, stamp_sum_own, picked_own, own_chosen, stamp_begin
    )


def solution(mesh):
    placed = (
        P(("groups", "vocab"), None),
        P("vocab", None),
        P(None, "groups"),
        P("groups"),
        P("groups"),
        P("groups"),
        P(None, "groups"),
    )
    return jax.shard_map(
        per_device,
        mesh=mesh,
        in_specs=placed,
        out_specs=(P(None, ("groups", "vocab")), P(("groups", "vocab"))),
        check_vma=False,
    )
```

profile of v0, /device:TPU:0, one launch (start us, length us, event | category | flops | bytes accessed | tf_op | source)
XLA Modules:
  0.0 115.1 jit_solution(743491746212821573)
XLA Ops:
  7.2 0.0 copy-start
  7.2 0.0 reduce-scatter.4.cloned.1.call-start
  7.3 0.0 copy-start.3
  7.3 0.7 copy-done.3
  8.0 0.0 copy-start.1
  8.0 25.3 %all_gather.3 = bf16[256,1280]{1,0:T(8,128)(2,1)S(1)} all-gather(bf16[16,1280]{1,0:T(8,128)(2,1)} %param.7), channel_id=1, replica_groups=mesh['groups'=2,'vocab'=16] {'vocab'}, dimensions={0}, use_global_device_ids=true | all-gather | bytes 696320 | tf_op jit(solution)/shard_map/all_gather | solution.py:75
  33.4 0.0 copy-done.1
  33.4 0.1 copy.19
  33.5 0.0 copy-start.4
  33.6 0.0 copy-start.5
  33.6 0.2 reshape.60
  33.8 0.0 copy-start.2
  33.8 0.4 copy-done.4
  34.2 0.0 copy-done.5
  34.2 0.2 copy-done.2
  34.5 0.0 copy-done
  34.5 0.7 select_reduce_fusion.1
  35.2 10.1 %gather_fusion = f32[1280]{0:T(1024)S(1)} fusion(f32[256,384]{1,0:T(8,128)S(1)} %get-tuple-element.59, s32[1280]{0:T(1024)S(1)} %reshape.60), kind=kCustom, calls=%fused_computation | custom fusion | bytes 20480 | tf_op jit(solution)/shard_map/while/body/eval_jaxpr/jit(take_along_axis)/gather | solution.py:60
  45.3 0.2 reshape.63
  45.5 0.1 copy.20
  45.6 0.8 copy.21
  46.4 0.0 reduce-scatter.4.cloned.1.call-update
  46.4 29.8 %all-reduce.1 = (f32[256]{0:T(256)S(1)}, f32[256]{0:T(256)S(1)}) all-reduce(f32[256]{0:T(256)S(1)} %get-tuple-element.31, f32[256]{0:T(256)S(1)} %get-tuple-element.30), channel_id=1, replica_groups=mesh['groups'=2,'vocab'=16] {'vocab'}, use_global_device_ids=true, to_apply=%region_2.3 | all-reduce | flops 512 | bytes 4096 | tf_op jit(solution)/shard_map/pmax | solution.py:109
  76.3 0.3 select_reduce_fusion
  76.6 29.5 %all-reduce = (f32[256]{0:T(256)S(1)}, f32[256]{0:T(256)S(1)}) all-reduce(f32[256]{0:T(256)S(1)} %exponential_multiply_fusion.1, f32[256]{0:T(256)S(1)} %exponential_multiply_fusion), channel_id=1, replica_groups=mesh['groups'=2,'vocab'=16] {'vocab'}, use_global_device_ids=true, to_apply=%region_4.5 | all-reduce | flops 512 | bytes 4096 | tf_op jit(solution)/shard_map/psum | solution.py:110
  106.1 0.6 subtract_maximum_fusion.1
  106.7 0.1 maximum_multiply_fusion
  106.8 0.0 reduce-scatter.4.cloned.1.call-done
  106.8 0.8 copy.22
  107.6 0.7 subtract_maximum_fusion
  (11 shorter events, 0.1 us)
Async XLA Ops:
  7.2 27.3 %copy-start = (bf16[384,1280]{1,0:T(8,128)(2,1)S(1)}, bf16[384,1280]{1,0:T(8,128)(2,1)}, u32[]{:S(2)}) copy-start(bf16[384,1280]{1,0:T(8,128)(2,1)} %param.8) | copy-start | bytes 2949124
  7.2 99.6 %reduce-scatter.4.cloned.1.call-start = ((), (), s32[]{:S(2)}) async-start(), calls=%async_computation.1 | async-start | bytes 139264
  7.3 0.8 copy-start.3
  8.0 25.3 %copy-start.1 = (s32[5,256]{1,0:T(8,128)S(1)}, s32[5,256]{1,0:T(8,128)}, u32[]{:S(2)}) copy-start(s32[5,256]{1,0:T(8,128)} %param.13) | copy-start | bytes 15364
  33.5 0.7 copy-start.4
  33.6 0.7 copy-start.5
  33.8 0.7 copy-start.2
Sparse Core Ops, SparseCore 0:
  46.6 52.9 reduce-scatter.3
where the time goes:
time: 115 us
  blocking collectives  84.7 us (74%)
  between operations  14.2 us (12%)
  local copies, waits for them, and re-layouts  13.7 us (12%)
  other arithmetic  1.76 us (2%)
    pmax x1, blocking collectives, per_device(): text_top, stamp_top = lax.pmax((text_max, stamp_max), 'vocab')  29.8 us
    psum x1, blocking collectives, per_device(): lax.psum((text_total * jnp.exp(text_max - text_top), stamp_total * jnp.ex...  29.5 us
    all_gather x1, blocking collectives, per_device(): piece = lax.all_gather(hidden, 'vocab', axis=0, tiled=True)  25.3 us
    gather x5, local copies, waits for them, and re-layouts, block_stats(): found = jnp.take_along_axis(values, local_pick.T, axis=1).T  10.7 us
    unnamed x14, local copies, waits for them, and re-layouts  2.98 us
  transfers between devices with their start and end apart: 1, of which 0 were waited for; matrix products, arithmetic and copies ran while one was open for 1% of the time, Pallas kernels for 0%

commit v1 on v0

v1 whole, which is shorter than its diff:
```python
import jax
import jax.numpy as jnp
from jax import lax
from jax.sharding import PartitionSpec as P

TSN = 1501
SPECIALS = 108
INITIAL = 50

MASK_VALUE = -1000000000.0
EMPTY_VALUE = -3000000000.0
SLOPE = 4.0
FLOOR = -30.0


def rule_mask(column, prev_tokens, last_stamp, sample_begin, seq_length, stamp_begin):
    generated = seq_length - sample_begin
    last_is = (generated >= 1) & (prev_tokens[1] >= stamp_begin)
    before_is = (generated < 2) | (prev_tokens[0] >= stamp_begin)
    both = last_is & before_is
    single = last_is & ~before_is
    is_stamp = column >= stamp_begin
    offset = column - stamp_begin
    masked = column == stamp_begin - 1
    masked = masked | both[None, :] & is_stamp
    masked = masked | single[None, :] & (column < stamp_begin - SPECIALS)
    bound = last_stamp + jnp.where(single, 0, 1).astype(jnp.int32)
    masked = masked | is_stamp & (offset < bound[None, :]) & (last_stamp >= 0)[None, :]
    begin = (generated == 0)[None, :]
    masked = masked | begin & (column < stamp_begin)
    masked = masked | begin & (offset > INITIAL)
    return masked


def shard_stats(rows, table, first_column, prev, stamp, begin, length, chosen, stamp_begin):
    width = table.shape[0]
    logits = lax.dot_general(
        table, rows, (((1,), (1,)), ((), ())), preferred_element_type=jnp.float32
    )
    column = first_column + lax.broadcasted_iota(jnp.int32, (width, 1), 0)
    is_text = column < stamp_begin
    masked = rule_mask(column, prev, stamp, begin, length, stamp_begin)
    values = jnp.where(masked, MASK_VALUE, logits)
    text_max = jnp.max(jnp.where(is_text, values, EMPTY_VALUE), axis=0)
    stamp_max = jnp.max(jnp.where(is_text, EMPTY_VALUE, values), axis=0)
    scaled = jnp.exp(values - jnp.where(is_text, text_max[None, :], stamp_max[None, :]))
    text_total = jnp.sum(jnp.where(is_text, scaled, 0.0), axis=0)
    stamp_total = jnp.sum(jnp.where(is_text, 0.0, scaled), axis=0)
    picked = [
        jnp.sum(jnp.where(column == chosen[k][None, :], values, 0.0), axis=0)
        for k in range(chosen.shape[0])
    ]
    text_lse = text_max + jnp.log(text_total)
    stamp_lse = stamp_max + jnp.log(stamp_total)
    return jnp.stack([text_max, text_lse, stamp_lse] + picked)


def merged_lse(parts):
    top = jnp.max(parts, axis=0)
    return top + jnp.log(jnp.sum(jnp.exp(parts - top[None, :]), axis=0))


def finalize(stats, chosen, stamp_begin):
    text_max = jnp.max(stats[:, 0], axis=0)
    text_lse = merged_lse(stats[:, 1])
    stamp_lse = merged_lse(stats[:, 2])
    picked = jnp.sum(stats[:, 3:], axis=0)
    penalty = SLOPE * jnp.maximum(stamp_lse - text_max, 0.0)
    shifted = text_lse - penalty
    larger = jnp.maximum(shifted, stamp_lse)
    total = larger + jnp.log(jnp.exp(shifted - larger) + jnp.exp(stamp_lse - larger))
    adjusted = picked - jnp.where(chosen < stamp_begin, penalty[None, :], 0.0) - total[None, :]
    return (jnp.maximum(adjusted, FLOOR), jnp.maximum(stamp_lse - total, FLOOR))


def per_device(hidden, embedding, prev_tokens, last_stamp, sample_begin, seq_length, chosen):
    width = embedding.shape[0]
    row_dev = hidden.shape[0]
    count = lax.axis_size("vocab")
    index = lax.axis_index("vocab")
    stamp_begin = width * count - TSN
    rows = lax.all_gather(hidden, "vocab", axis=0, tiled=True)
    stats = shard_stats(
        rows, embedding, index * width, prev_tokens, last_stamp, sample_begin, seq_length,
        chosen, stamp_begin,
    )
    fields = stats.shape[0]
    sent = stats.reshape(fields, count, row_dev).transpose(1, 0, 2)
    got = lax.all_to_all(sent, "vocab", 0, 0, tiled=True)
    own_chosen = lax.dynamic_slice_in_dim(chosen, index * row_dev, row_dev, 1)
    return finalize(got, own_chosen, stamp_begin)


def solution(mesh):
    placed = (
        P(("groups", "vocab"), None),
        P("vocab", None),
        P(None, "groups"),
        P("groups"),
        P("groups"),
        P("groups"),
        P(None, "groups"),
    )
    return jax.shard_map(
        per_device,
        mesh=mesh,
        in_specs=placed,
        out_specs=(P(None, ("groups", "vocab")), P(("groups", "vocab"))),
        check_vma=False,
    )
```

time: 115 us -> 42.9 us (0.37)
  blocking collectives: 84.7 us -> 25.3 us
  between operations: 14.2 us -> 0.79 us
  local copies, waits for them, and re-layouts: 13.7 us -> 3.55 us
  waiting for transfers between devices: 0.02 us -> 6.4 us
  starting transfers between devices: 0.04 us -> 3.49 us
    pmax x1 -> x0, blocking collectives: 29.8 us -> none  [per_device(): text_top, stamp_top = lax.pmax((text_max, stamp_max), 'vocab')]
    psum x1 -> x0, blocking collectives: 29.5 us -> none  [per_device(): lax.psum((text_total * jnp.exp(text_max - text_top), stamp_total * jnp.ex...]
    gather x5 -> x0, local copies, waits for them, and re-layouts: 10.7 us -> none  [block_stats(): found = jnp.take_along_axis(values, local_pick.T, axis=1).T]
    all_to_all x0 -> x1, waiting for transfers between devices: none -> 6.4 us  [per_device(): got = lax.all_to_all(sent, 'vocab', 0, 0, tiled=True)]
    all_to_all x0 -> x1, starting transfers between devices: none -> 3.49 us  [per_device(): got = lax.all_to_all(sent, 'vocab', 0, 0, tiled=True)]
  transfers between devices with their start and end apart: 1 -> 1, of which waited for: 0 -> 1; matrix products, arithmetic and copies ran while one was open for 1% -> 0% of each run, Pallas kernels for 0% -> 0%
where the time goes in v1:
time: 42.9 us; the launch traced here: 42.6 us
  blocking collectives  25.3 us (59%)
  waiting for transfers between devices  6.4 us (15%)
  local copies, waits for them, and re-layouts  3.55 us (8%)
  starting transfers between devices  3.49 us (8%)
  other arithmetic  2.49 us (6%)
  between operations  0.79 us (2%)
  matrix products  0.56 us (1%)
    all_gather x1, blocking collectives, per_device(): rows = lax.all_gather(hidden, 'vocab', axis=0, tiled=True)  25.3 us
    all_to_all x1, waiting for transfers between devices, per_device(): got = lax.all_to_all(sent, 'vocab', 0, 0, tiled=True)  6.4 us
    all_to_all x1, starting transfers between devices, per_device(): got = lax.all_to_all(sent, 'vocab', 0, 0, tiled=True)  3.49 us
    unnamed x14, local copies, waits for them, and re-layouts  2.2 us
    max x2, other arithmetic, finalize(): return (jnp.maximum(adjusted, FLOOR), jnp.maximum(stamp_lse - total, FLOOR))  1.22 us
  transfers between devices with their start and end apart: 1, of which 1 were waited for; matrix products, arithmetic and copies ran while one was open for 0% of the time, Pallas kernels for 0%

profile of v1, /device:TPU:0, one launch (start us, length us, event | category | flops | bytes accessed | tf_op | source)
XLA Modules:
  0.0 42.6 jit_solution(8149360842820527205)
XLA Ops:
  0.6 0.0 copy-start
  0.7 0.0 copy-start.3
  0.7 0.7 %copy-done.3 = s32[2,256]{1,0:T(2,128)S(1)} copy-done((s32[2,256]{1,0:T(2,128)S(1)}, s32[2,256]{1,0:T(2,128)}, u32[]{:S(2)}) %copy-start.3) | copy-done | bytes 2072
  1.5 0.0 copy-start.1
  1.5 25.3 %all_gather.3 = bf16[256,1280]{1,0:T(8,128)(2,1)S(1)} all-gather(bf16[16,1280]{1,0:T(8,128)(2,1)} %param.7), channel_id=1, replica_groups=mesh['groups'=2,'vocab'=16] {'vocab'}, dimensions={0}, use_global_device_ids=true | all-gather | bytes 696320 | tf_op jit(solution)/shard_map/all_gather | solution.py:82
  26.8 0.0 copy-done.1
  26.8 0.0 copy-start.4
  26.8 0.0 copy-start.5
  26.8 0.0 copy-start.2
  26.8 0.7 %copy-done.4 = s32[256]{0:T(256)S(1)} copy-done((s32[256]{0:T(256)S(1)}, s32[256]{0:T(256)}, u32[]{:S(2)}) %copy-start.4) | copy-done | bytes 1048
  27.5 0.0 copy-done.5
  27.5 0.0 copy-done.2
  27.6 0.0 copy-done
  27.6 0.6 %select_reduce_fusion.7 = (f32[256]{0:T(256)S(1)}, f32[256]{0:T(256)S(1)}, f32[384,256]{1,0:T(8,128)S(1)}) fusion(pred[384]{0:T(512)(128)(4,1)S(1)} %get-tuple-element.40, bf16[384,1280]{1,0:T(8,128)(2,1)S(1)} %copy-done, bf16[256,1280]{1,0:T(8,128)(2,1)S(1)} %all_gather.3, pred[384]{0:T(512)(128)(4,1)S(1)} %broadcast_compare_fusion, ...), kind=kOutput, calls=%fused_computation.9 | convolution fusion | flops 253328896 | bytes 2039168 | tf_op jit(solution)/shard_map/dot_general | solution.py:37
  28.1 0.1 stack.23
  28.2 0.4 select_reduce_fusion
  28.6 0.1 add.105
  28.7 0.1 log.51
  28.8 0.1 stack.24
  28.9 0.1 stack.25
  29.0 0.1 stack.26
  29.1 0.1 stack.27
  29.2 0.1 stack.28
  29.3 0.1 stack.29
  29.4 0.7 %reshape.136 = f32[16,1,128]{2,1,0:T(1,128)} reshape(f32[16,8,16]{2,1,0:T(8,128)S(1)} %bitcast.10) | data formatting | bytes 16384
  30.1 3.5 %all-to-all-start = ((f32[16,1,128]{2,1,0:T(1,128)}), f32[16,1,128]{2,1,0:T(1,128)S(1)}, u32[]{:S(2)}, u32[]{:S(2)}) async-start(f32[16,1,128]{2,1,0:T(1,128)} %reshape.136), calls=%async_computation | async-start | bytes 16384 | tf_op jit(solution)/shard_map/all_to_all | solution.py:89
  33.6 6.4 %all-to-all-done = f32[16,1,128]{2,1,0:T(1,128)S(1)} async-done(((f32[16,1,128]{2,1,0:T(1,128)}), f32[16,1,128]{2,1,0:T(1,128)S(1)}, u32[]{:S(2)}, u32[]{:S(2)}) %all-to-all-start) | async-done | bytes 8224 | tf_op jit(solution)/shard_map/all_to_all | solution.py:89
  40.0 0.5 %broadcast.125 = f32[]{:T(128)} broadcast(f32[]{:T(128)} %constant.64), dimensions={} | broadcast | bytes 8 | tf_op jit(solution)/shard_map/all_to_all | solution.py:89
  40.5 0.7 %reduce.7 = f32[16,128]{1,0:T(8,128)S(1)} reduce(f32[16,1,128]{2,1,0:T(1,128)S(1)} %all-to-all-done, f32[]{:T(128)} %broadcast.125), dimensions={1}, to_apply=%all_to_all.3.reduce_sub_computation | reduce | bytes 16388 | tf_op jit(solution)/shard_map/all_to_all | solution.py:89
  41.2 0.1 reshape.137
  41.4 0.6 %subtract_maximum_fusion.1 = (f32[16]{0:T(128)}, f32[16]{0:T(128)S(1)}, f32[16]{0:T(128)S(1)}) fusion(f32[16]{0:T(128)S(1)} %get-tuple-element.13, f32[16]{0:T(128)S(1)} %exponential_reduce_fusion.1, f32[16]{0:T(128)S(1)} %get-tuple-element.15, f32[16]{0:T(128)S(1)} %get-tuple-element.14, f32[16]{0:T(128)S(1)} %exponential_reduce_fusion), kind=kLoop, calls=%fused_computation.31 | loop fusion | flops 208 | bytes 512 | tf_op jit(solution)/shard_map/max | solution.py:73
  42.0 0.7 %subtract_maximum_fusion = f32[5,16]{1,0:T(8,128)} fusion(f32[5,16]{1,0:T(8,128)S(1)} %slice_reduce_fusion, s32[5,256]{1,0:T(8,128)S(1)} %copy-done.1, s32[]{:T(128)S(6)} %select_n.61, f32[16]{0:T(128)S(1)} %get-tuple-element.19, f32[16]{0:T(128)S(1)} %get-tuple-element.33), kind=kLoop, calls=%fused_computation.15 | loop fusion | flops 400 | bytes 1092 | tf_op jit(solution)/shard_map/max | solution.py:73
  (15 shorter events, 0.2 us)
Async XLA Ops:
  0.6 26.9 %copy-start = (bf16[384,1280]{1,0:T(8,128)(2,1)S(1)}, bf16[384,1280]{1,0:T(8,128)(2,1)}, u32[]{:S(2)}) copy-start(bf16[384,1280]{1,0:T(8,128)(2,1)} %param.8) | copy-start | bytes 2949124
  0.7 0.8 %copy-start.3 = (s32[2,256]{1,0:T(2,128)S(1)}, s32[2,256]{1,0:T(2,128)}, u32[]{:S(2)}) copy-start(s32[2,256]{1,0:T(2,128)} %param.9) | copy-start | bytes 6148
  1.5 25.3 %copy-start.1 = (s32[5,256]{1,0:T(8,128)S(1)}, s32[5,256]{1,0:T(8,128)}, u32[]{:S(2)}) copy-start(s32[5,256]{1,0:T(8,128)} %param.13) | copy-start | bytes 15364
  26.8 0.7 %copy-start.4 = (s32[256]{0:T(256)S(1)}, s32[256]{0:T(256)}, u32[]{:S(2)}) copy-start(s32[256]{0:T(256)} %param.12) | copy-start | bytes 3076
  26.8 0.7 %copy-start.5 = (s32[256]{0:T(256)S(1)}, s32[256]{0:T(256)}, u32[]{:S(2)}) copy-start(s32[256]{0:T(256)} %param.11) | copy-start | bytes 3076
  26.8 0.7 %copy-start.2 = (s32[256]{0:T(256)S(1)}, s32[256]{0:T(256)}, u32[]{:S(2)}) copy-start(s32[256]{0:T(256)} %param.10) | copy-start | bytes 3076
  30.1 9.9 %all-to-all-start = ((f32[16,1,128]{2,1,0:T(1,128)}), f32[16,1,128]{2,1,0:T(1,128)S(1)}, u32[]{:S(2)}, u32[]{:S(2)}) async-start(f32[16,1,128]{2,1,0:T(1,128)} %reshape.136), calls=%async_computation | async-start | bytes 16384 | tf_op jit(solution)/shard_map/all_to_all | solution.py:89
